TPU v7x, 32 devices: a whole 2x2x4 slice. The times are simulated.
32 devices in a mesh: seq: 4 (over z), tp: 4 (over y, x), dp: 2 (over core).
Axes of the slice: x: 2, y: 2, z: 4, core: 2. Of those that a mesh axis runs over, the one named last changes fastest.
Arguments:
- x_ckpt: bfloat16 [1024, 5120], P(('dp', 'seq', 'tp')), parts along dimension 0, may hold values from -5 to 5
- bc_ckpt: bfloat16 [2, 1024, 128], P(None, ('dp', 'seq', 'tp')), parts along dimension 1, may hold values from -1 to 1
- step_sizes: float32 [80, 1024], P('tp', ('dp', 'seq')), parts along dimension 1, may hold values from 0.03 to 0.3
- decay_rate: float32 [80], P('tp'), may hold values from 0 to 1, as said below
- skip_gain: float32 [80], P('tp'), may hold values from 0.25 to 1.75
- grad_out: bfloat16 [1024, 5120], P(('dp', 'seq'), 'tp'), parts along dimension 0, may hold values from -3 to 3
Outputs:
- grad_x: bfloat16 [1024, 5120], P(('dp', 'seq'), 'tp'), parts along dimension 0
- grad_bc: float32 [2, 1024, 128], P(None, ('dp', 'seq', 'tp')), parts along dimension 1
- grad_step: float32 [80, 1024], P('tp', ('dp', 'seq')), parts along dimension 1
There are 2 independent parts, one for each index of `dp`. A program takes and returns all parts, laid end to end along the dimension named above; an argument that names none is the same for every part. Nothing has to cross between parts.
Inputs may be any that keep to these rules, and one draw needn't show every extreme that they name: `decay_rate`: positive decay rates of the 80 heads.
All inputs are finite; a program needn't handle non-finite values.
Results may differ from a plain program's by a relative error of at most 0.001.
Values may be sent and summed in bfloat16 or wider, within the bound.
No kernel may reach another device: no remote copies, remote signals or barrier semaphores. Data moves between devices by JAX's collectives and lax.ppermute only.
A program may use at most 128 MiB of HBM per device.

v0:
```python
from functools import partial
import jax
import jax.numpy as jnp
from jax import lax
from jax.sharding import PartitionSpec as P

BLOCK = 128
highest = lax.Precision.HIGHEST


def carried_in(array, axis, combine, identity, reverse):
    peers, index = (lax.axis_size(axis), lax.axis_index(axis))
    everything = jax.tree.map(lambda part: lax.all_gather(part, axis), array)
    start = jax.tree.map(
        lambda part, zero: jnp.broadcast_to(jnp.asarray(zero, part.dtype), part.shape),
        array,
        identity,
    )

    def hop(k, before):
        at = peers - 1 - k if reverse else k
        reached = at > index if reverse else at < index
        new = combine(before, jax.tree.map(lambda part: part[at], everything))
        return jax.tree.map(lambda a, b: jnp.where(reached, a, b), new, before)

    return lax.fori_loop(0, peers, hop, start)


def block_step(head_rates, head_gains, carry_state, pieces):
    inputs, step_block, proj_b, proj_c = pieces
    head_count = step_block.shape[0]
    row_count = step_block.shape[1]
    values = inputs.astype(jnp.float32).reshape(row_count, head_count, -1)
    cumulative = jnp.cumsum(-head_rates[:, None] * step_block, axis=1)
    positions = jnp.arange(row_count, dtype=jnp.int32)
    causal = positions[:, None] >= positions[None, :]
    log_gaps = cumulative[:, :, None] - cumulative[:, None, :]
    within = jnp.where(causal, jnp.exp(jnp.where(causal, log_gaps, 0.0)), 0.0)
    scores = jnp.dot(proj_c, proj_b.T, precision=highest, preferred_element_type=jnp.float32)
    weights = within * scores[None, :, :] * step_block[:, None, :]
    local_part = jnp.einsum(
        "hts,shp->thp", weights, values, precision=highest, preferred_element_type=jnp.float32
    )
    carried = jnp.einsum(
        "tn,hpn->thp", proj_c, carry_state, precision=highest, preferred_element_type=jnp.float32
    )
    carried = carried * jnp.exp(cumulative).T[:, :, None]
    result = local_part + carried + head_gains[None, :, None] * values
    tail_weight = jnp.exp(cumulative[:, -1:] - cumulative) * step_block
    fresh_state = jnp.einsum(
        "hs,shp,sn->hpn",
        tail_weight,
        values,
        proj_b,
        precision=highest,
        preferred_element_type=jnp.float32,
    )
    final_state = jnp.exp(cumulative[:, -1])[:, None, None] * carry_state + fresh_state
    return (final_state, result.reshape(row_count, -1))


def run_blocks(inputs, step_sizes, proj_b, proj_c, start_state, head_rates, head_gains, block_rows):
    row_count = inputs.shape[0]
    block_count = row_count // block_rows
    head_count = step_sizes.shape[0]
    input_blocks = inputs.reshape(block_count, block_rows, inputs.shape[1])
    step_blocks = step_sizes.reshape(head_count, block_count, block_rows).transpose(1, 0, 2)
    b_blocks = proj_b.reshape(block_count, block_rows, proj_b.shape[1])
    c_blocks = proj_c.reshape(block_count, block_rows, proj_c.shape[1])
    stepper = jax.checkpoint(partial(block_step, head_rates, head_gains))
    final_state, results = lax.scan(
        stepper, start_state, (input_blocks, step_blocks, b_blocks, c_blocks)
    )
    return (results.reshape(row_count, -1), final_state)


def combine(earlier, later):
    return (earlier[0] * later[0], later[0][:, None, None] * earlier[1] + later[1])


def shards(x_ckpt, bc_ckpt, step_sizes, decay_rate, skip_gain, grad_out):
    head_count = decay_rate.shape[0]
    width = grad_out.shape[1]
    own_rows = lax.all_to_all(x_ckpt, "tp", split_axis=1, concat_axis=0, tiled=True)
    pairs = lax.all_gather(bc_ckpt, "tp", axis=1, tiled=True)
    proj_b = pairs[0].astype(jnp.float32)
    proj_c = pairs[1].astype(jnp.float32)
    token_count = own_rows.shape[0]
    head_width = width // head_count
    values = own_rows.astype(jnp.float32).reshape(token_count, head_count, head_width)
    cumulative = jnp.cumsum(-decay_rate[:, None] * step_sizes, axis=1)
    passing = jnp.exp(cumulative[:, -1])
    tail_weight = jnp.exp(cumulative[:, -1:] - cumulative) * step_sizes
    summary = jnp.einsum(
        "hs,shp,sn->hpn",
        tail_weight,
        values,
        proj_b,
        precision=highest,
        preferred_element_type=jnp.float32,
    )
    upstream = grad_out.astype(jnp.float32)
    pulled = jnp.einsum(
        "ht,thp,tn->hpn",
        jnp.exp(cumulative),
        upstream.reshape(token_count, head_count, head_width),
        proj_c,
        precision=highest,
        preferred_element_type=jnp.float32,
    )
    neutral = (jnp.ones_like(passing), jnp.zeros_like(summary))
    entering = carried_in((passing, summary), "seq", combine, neutral, False)[1]
    leaving = carried_in((passing, pulled), "seq", combine, neutral, True)[1]

    def forward(inputs, basis_b, basis_c, step_block, start_state):
        return run_blocks(
            inputs, step_block, basis_b, basis_c, start_state, decay_rate, skip_gain, BLOCK
        )

    outputs, pull_back = jax.vjp(forward, own_rows, proj_b, proj_c, step_sizes, entering)
    grad_x, grad_b, grad_c, grad_step, unused = pull_back((upstream, leaving))
    partial_grads = jnp.stack([grad_b, grad_c])
    grad_bc = lax.psum_scatter(partial_grads, "tp", scatter_dimension=1, tiled=True)
    return (grad_x, grad_bc, grad_step)


def solution(mesh):
    return jax.shard_map(
        shards,
        mesh=mesh,
        in_specs=(
            P(("dp", "seq", "tp"), None),
            P(None, ("dp", "seq", "tp"), None),
            P("tp", ("dp", "seq")),
            P("tp"),
            P("tp"),
            P(("dp", "seq"), "tp"),
        ),
        out_specs=(
            P(("dp", "seq"), "tp"),
            P(None, ("dp", "seq", "tp"), None),
            P("tp", ("dp", "seq")),
        ),
        check_vma=False,
    )
```

profile of v0, /device:TPU:0, one launch (start us, length us, event | category | flops | bytes accessed | tf_op | source)
XLA Modules:
  0.0 178.6 jit_solution(7967003669195045583)
XLA Ops:
  7.9 0.8 broadcast_multiply_fusion.2
  9.1 0.8 exponential_bitcast_fusion
  9.9 9.9 %all_gather.22 = bf16[2,128,128]{2,1,0:T(8,128)(2,1)S(1)} all-gather(bf16[2,32,128]{2,1,0:T(8,128)(2,1)} %param.11), channel_id=1, replica_groups=mesh['seq'=4,'tp'=4,'dp'=2] {'tp'}, dimensions={1}, use_global_device_ids=true | all-gather | bytes 81920 | tf_op jit(solution)/shard_map/all_gather | solution.py:85
  19.8 1.2 copy.35
  21.1 1.3 fusion.32
  22.4 0.7 copy.53
  23.1 3.5 %all-to-all-start = ((bf16[32,4,1280]{2,0,1:T(8,128)(2,1)}), bf16[32,4,1280]{2,0,1:T(8,128)(2,1)S(1)}, u32[]{:S(2)}, u32[]{:S(2)}) async-start(bf16[32,4,1280]{2,0,1:T(8,128)(2,1)} %bitcast.97), calls=%async_computation | async-start | bytes 655360 | tf_op jit(solution)/shard_map/all_to_all | solution.py:84
  26.7 5.4 %all-to-all-done = bf16[32,4,1280]{2,0,1:T(8,128)(2,1)S(1)} async-done(((bf16[32,4,1280]{2,0,1:T(8,128)(2,1)}), bf16[32,4,1280]{2,0,1:T(8,128)(2,1)S(1)}, u32[]{:S(2)}, u32[]{:S(2)}) %all-to-all-start) | async-done | bytes 327712 | tf_op jit(solution)/shard_map/all_to_all | solution.py:84
  33.3 2.0 %fusion.2 = f32[20,64,128]{2,1,0:T(8,128)} fusion(f32[128,20,64]{2,1,0:T(8,128)S(1)} %broadcast_multiply_fusion, bf16[2,128,128]{2,1,0:T(8,128)(2,1)S(1)} %all_gather.22), kind=kOutput, calls=%fused_computation.6 | convolution fusion | flops 251658240 | bytes 2260992 | tf_op jit(solution)/shard_map/hs,shp,sn->hpn/dot_general | solution.py:94
  37.0 12.7 %all-reduce.2 = f32[80]{0:T(128)S(1)} all-reduce(f32[80]{0:T(128)S(1)} %dynamic-update-slice), channel_id=2, replica_groups=mesh['seq'=4,'tp'=4,'dp'=2] {'seq'}, use_global_device_ids=true, to_apply=%add.2 | all-reduce | flops 80 | bytes 640
  49.8 0.8 bitcast_convert_fusion.1
  50.6 27.2 %all-gather.8.cloned.1.call-done = f32[80,64,128]{2,1,0:T(8,128)} async-done(((f32[20,64,128]{2,1,0:T(8,128)}), f32[80,64,128]{2,1,0:T(8,128)}) %all-gather.8.cloned.1.call-update) | async-done | bytes 2621456 | tf_op jit(solution)/shard_map/all_gather | solution.py:13
  77.7 5.1 %while.21 = (s32[]{:T(128)}, f32[20,64,128]{2,1,0:T(8,128)S(1)}, s32[]{:T(128)}, f32[4,20]{1,0:T(4,128)S(1)}, f32[4,20,64,128]{3,2,1,0:T(8,128)}, /*index=5*/s32[]{:T(128)}, s32[]{:T(128)}, s32[]{:T(128)}, s32[]{:T(128)}) while((s32[]{:T(128)}, f32[20,64,128]{2,1,0:T(8,128)S(1)}, s32[]{:T(128)}, f32[4,20]{1,0:T(4,128)S(1)}, ...), condition=%wide.region_4.5_spmd.clone, body=%wide.region_3.4_spmd.clone.sunk | while | flops 655368 | bytes 1966487 | solution.py:26
  77.8 1.2 fusion.67
  79.0 1.2 fusion.67
  80.3 1.2 fusion.67
  81.6 1.2 fusion.67
  82.8 50.0 %all-gather.6.cloned.1.call-done = f32[80,64,128]{2,1,0:T(8,128)} async-done(((f32[20,64,128]{2,1,0:T(8,128)}), f32[80,64,128]{2,1,0:T(8,128)}) %all-gather.6.cloned.1.call-update) | async-done | bytes 2621456 | tf_op jit(solution)/shard_map/all_gather | solution.py:13
  132.8 5.1 %while.20 = (s32[]{:T(128)}, f32[20,64,128]{2,1,0:T(8,128)S(1)}, s32[]{:T(128)}, f32[4,20]{1,0:T(4,128)S(1)}, f32[4,20,64,128]{3,2,1,0:T(8,128)}, /*index=5*/s32[]{:T(128)}, s32[]{:T(128)}) while((s32[]{:T(128)}, f32[20,64,128]{2,1,0:T(8,128)S(1)}, s32[]{:T(128)}, f32[4,20]{1,0:T(4,128)S(1)}, f32[4,20,64,128]{3,2,1,0:T(8,128)}, ...), condition=%wide.region_2.3_spmd.clone, body=%wide.region_1.2_spmd.clone.sunk | while | flops 655364 | bytes 1966425 | solution.py:26
  132.8 1.2 fusion.66
  134.1 1.2 fusion.66
  135.4 1.2 fusion.66
  136.7 1.2 fusion.66
  139.3 0.7 fusion.23
  140.5 0.7 fusion.18
  141.2 2.2 %fusion.22 = (f32[20,128]{1,0:T(8,128)S(1)}, f32[20,128]{1,0:T(8,128)S(1)}, f32[20,128]{1,0:T(8,128)S(1)}, f32[128,128]{1,0:T(8,128)S(1)}) fusion(f32[20,128]{1,0:T(8,128)S(1)} %copy-done.4, f32[128,128]{1,0:T(8,128)S(1)} %fusion.50, f32[20,128]{1,0:T(8,128)S(1)} %reduce_window_sum.35, pred[128,128]{1,0:T(8,128)(4,1)S(1)} %iota_compare_fusion, ...), kind=kOutput, calls=%fused_computation.29 | convolution fusion | flops 256549376 | bytes 1181696 | tf_op jit(solution)/shard_map/transpose(jvp())/while/body/eval_jaxpr/checkpoint/hts,shp->thp/dot_general | solution.py:41
  143.5 1.2 convolution_bitcast_fusion.1
  144.7 1.2 reduce_window_sum.36
  146.6 1.2 convolution_bitcast_fusion
  149.0 1.6 fusion.15
  150.7 0.9 copy.39
  151.6 20.5 %reduce-scatter.2.cloned.1.call-done = f32[2,32,128]{2,1,0:T(8,128)} async-done(((f32[2,128,128]{2,1,0:T(8,128)}), f32[2,32,128]{2,1,0:T(8,128)}) %reduce-scatter.2.cloned.1.call-update) | async-done | bytes 32784 | tf_op jit(solution)/shard_map/reduce_scatter | solution.py:123
  (60 shorter events, 7.4 us)
Async XLA Ops:
  7.2 70.6 %all-gather.8.cloned.1.call-start = ((), (), s32[]{:S(2)}) async-start(), calls=%async_computation.4 | async-start | bytes 3276800 | tf_op jit(solution)/shard_map/all_gather | solution.py:13
  19.8 13.5 %copy-start.2 = (bf16[2,128,128]{2,1,0:T(8,128)(2,1)}, bf16[2,128,128]{2,1,0:T(8,128)(2,1)S(1)}, u32[]{:S(2)}) copy-start(bf16[2,128,128]{2,1,0:T(8,128)(2,1)S(1)} %all_gather.22) | copy-start | bytes 196612
  21.0 1.4 copy-start.3
  23.1 9.0 %all-to-all-start = ((bf16[32,4,1280]{2,0,1:T(8,128)(2,1)}), bf16[32,4,1280]{2,0,1:T(8,128)(2,1)S(1)}, u32[]{:S(2)}, u32[]{:S(2)}) async-start(bf16[32,4,1280]{2,0,1:T(8,128)(2,1)} %bitcast.97), calls=%async_computation | async-start | bytes 655360 | tf_op jit(solution)/shard_map/all_to_all | solution.py:84
  26.6 106.2 %all-gather.6.cloned.1.call-start = ((), (), s32[]{:S(2)}) async-start(), calls=%async_computation.3 | async-start | bytes 3276800 | tf_op jit(solution)/shard_map/all_gather | solution.py:13
  32.1 0.7 copy-start
  33.3 2.2 %copy-start.7 = (u32[32]{0:T(128)S(1)}, u32[32]{0:T(128)}, u32[]{:S(2)}) copy-start(u32[32]{0:T(128)} %constant.131) | copy-start | bytes 388
  35.4 136.7 %reduce-scatter.2.cloned.1.call-start = ((), (), s32[]{:S(2)}) async-start(), calls=%async_computation.2 | async-start | bytes 163840 | tf_op jit(solution)/shard_map/reduce_scatter | solution.py:123
  132.8 5.1 %copy-start.5 = (f32[20]{0:T(128)S(1)}, f32[20]{0:T(128)}, u32[]{:S(2)}) copy-start(f32[20]{0:T(128)} %param.13) | copy-start | bytes 244
  132.8 5.1 %copy-start.4 = (f32[20,128]{1,0:T(8,128)S(1)}, f32[20,128]{1,0:T(8,128)}, u32[]{:S(2)}) copy-start(f32[20,128]{1,0:T(8,128)} %param.12) | copy-start | bytes 30724
  137.9 1.0 copy-start.1
  144.7 4.3 %copy-start.6 = (f32[20]{0:T(128)S(1)}, f32[20]{0:T(128)}, u32[]{:S(2)}) copy-start(f32[20]{0:T(128)} %param.14) | copy-start | bytes 244
Sparse Core Ops, SparseCore 0:
  22.5 55.2 all-gather.7
  79.3 53.4 all-gather.5
  149.2 22.8 reduce-scatter.1
where the time goes:
time: 179 us
  waiting for transfers between devices  103 us (58%)
  blocking collectives  22.6 us (13%)
  other arithmetic  17.4 us (10%)
  between operations  14.6 us (8%)
  matrix products  11.7 us (7%)
  local copies, waits for them, and re-layouts  5.46 us (3%)
  starting transfers between devices  3.58 us (2%)
    all_gather x2, waiting for transfers between devices, carried_in(): everything = jax.tree.map(lambda part: lax.all_gather(part, axis), array)  77.2 us
    reduce_scatter x1, waiting for transfers between devices, shards(): lax.psum_scatter(partial_grads, 'tp', scatter_dimension=1, tiled=True)  20.5 us
    unnamed x1, blocking collectives  12.7 us
    all_gather x1, blocking collectives, shards(): pairs = lax.all_gather(bc_ckpt, 'tp', axis=1, tiled=True)  9.88 us
    select_n x8, other arithmetic, hop(): return jax.tree.map(lambda a, b: jnp.where(reached, a, b), new, before)  9.87 us
    all_to_all x1, waiting for transfers between devices, shards(): lax.all_to_all(x_ckpt, 'tp', split_axis=1, concat_axis=0, tiled=True)  5.35 us
    dot_general x2, matrix products, block_step(): jnp.einsum('hts,shp->thp', weights, values, precision=highest, preferred_...  3.77 us
  transfers between devices with their start and end apart: 4, of which 4 were waited for; matrix products, arithmetic and copies ran while one was open for 7% of the time, Pallas kernels for 0%

commit v1 on v0

--- a/solution.py
+++ b/solution.py
@@ -81,7 +81,10 @@
 def shards(x_ckpt, bc_ckpt, step_sizes, decay_rate, skip_gain, grad_out):
     head_count = decay_rate.shape[0]
     width = grad_out.shape[1]
-    own_rows = lax.all_to_all(x_ckpt, "tp", split_axis=1, concat_axis=0, tiled=True)
+    own_rows = jnp.concatenate(
+        lax.all_to_all(jnp.stack(jnp.split(x_ckpt, lax.axis_size("tp"), axis=1)), "tp", 0, 0),
+        axis=0,
+    )
     pairs = lax.all_gather(bc_ckpt, "tp", axis=1, tiled=True)
     proj_b = pairs[0].astype(jnp.float32)
     proj_c = pairs[1].astype(jnp.float32)

time: 179 us -> 180 us (level)
  no operation moved by 1% of the time
where the time goes in v1:
time: 180 us; the launch traced here: 179 us
  waiting for transfers between devices  103 us (57%)
  blocking collectives  22.6 us (13%)
  other arithmetic  18.1 us (10%)
  between operations  14.6 us (8%)
  matrix products  11.7 us (6%)
  local copies, waits for them, and re-layouts  4.64 us (3%)
  starting transfers between devices  3.58 us (2%)
    all_gather x2, waiting for transfers between devices, carried_in(): everything = jax.tree.map(lambda part: lax.all_gather(part, axis), array)  77.3 us
    reduce_scatter x1, waiting for transfers between devices, shards(): lax.psum_scatter(partial_grads, 'tp', scatter_dimension=1, tiled=True)  20.5 us
    unnamed x1, blocking collectives  12.7 us
    all_gather x1, blocking collectives, shards(): pairs = lax.all_gather(bc_ckpt, 'tp', axis=1, tiled=True)  9.88 us
    select_n x8, other arithmetic, hop(): return jax.tree.map(lambda a, b: jnp.where(reached, a, b), new, before)  9.86 us
    all_to_all x1, waiting for transfers between devices, shards(): lax.all_to_all(jnp.stack(jnp.split(x_ckpt, lax.axis_size('tp'), axis=1)),...  5.35 us
    dot_general x2, matrix products, block_step(): jnp.einsum('hts,shp->thp', weights, values, precision=highest, preferred_...  3.74 us
  transfers between devices with their start and end apart: 4, of which 4 were waited for; matrix products, arithmetic and copies ran while one was open for 7% of the time, Pallas kernels for 0%

profile of v1, /device:TPU:0, one launch (start us, length us, event | category | flops | bytes accessed | tf_op | source)
XLA Modules:
  0.0 178.7 jit_solution(18374866715695577578)
XLA Ops:
  7.9 0.8 broadcast_multiply_fusion.2
  9.1 0.8 exponential_bitcast_fusion
  9.9 9.9 %all_gather.22 = bf16[2,128,128]{2,1,0:T(8,128)(2,1)S(1)} all-gather(bf16[2,32,128]{2,1,0:T(8,128)(2,1)} %param.11), channel_id=1, replica_groups=mesh['seq'=4,'tp'=4,'dp'=2] {'tp'}, dimensions={1}, use_global_device_ids=true | all-gather | bytes 81920 | tf_op jit(solution)/shard_map/all_gather | solution.py:88
  19.8 1.2 copy.25
  21.1 1.3 fusion.32
  22.4 0.8 pad_maximum_fusion
  23.2 3.5 %all-to-all-start = ((bf16[4,32,1280]{2,1,0:T(8,128)(2,1)}), bf16[4,32,1280]{2,1,0:T(8,128)(2,1)S(1)}, u32[]{:S(2)}, u32[]{:S(2)}) async-start(bf16[4,32,1280]{2,1,0:T(8,128)(2,1)} %pad_maximum_fusion), calls=%async_computation | async-start | bytes 655360 | tf_op jit(solution)/shard_map/all_to_all | solution.py:85
  26.8 5.4 %all-to-all-done = bf16[4,32,1280]{2,1,0:T(8,128)(2,1)S(1)} async-done(((bf16[4,32,1280]{2,1,0:T(8,128)(2,1)}), bf16[4,32,1280]{2,1,0:T(8,128)(2,1)S(1)}, u32[]{:S(2)}, u32[]{:S(2)}) %all-to-all-start) | async-done | bytes 327712 | tf_op jit(solution)/shard_map/all_to_all | solution.py:85
  33.1 2.0 %fusion.2 = f32[20,64,128]{2,1,0:T(8,128)} fusion(f32[128,20,64]{2,1,0:T(8,128)S(1)} %broadcast_multiply_fusion, bf16[2,128,128]{2,1,0:T(8,128)(2,1)S(1)} %all_gather.22), kind=kOutput, calls=%fused_computation.6 | convolution fusion | flops 251658240 | bytes 2260992 | tf_op jit(solution)/shard_map/hs,shp,sn->hpn/dot_general | solution.py:97
  36.8 12.7 %all-reduce.2 = f32[80]{0:T(128)S(1)} all-reduce(f32[80]{0:T(128)S(1)} %dynamic-update-slice), channel_id=2, replica_groups=mesh['seq'=4,'tp'=4,'dp'=2] {'seq'}, use_global_device_ids=true, to_apply=%add.2 | all-reduce | flops 80 | bytes 640
  49.6 0.8 bitcast_convert_fusion
  50.4 27.4 %all-gather.8.cloned.1.call-done = f32[80,64,128]{2,1,0:T(8,128)} async-done(((f32[20,64,128]{2,1,0:T(8,128)}), f32[80,64,128]{2,1,0:T(8,128)}) %all-gather.8.cloned.1.call-update) | async-done | bytes 2621456 | tf_op jit(solution)/shard_map/all_gather | solution.py:13
  77.8 5.1 %while.21 = (s32[]{:T(128)}, f32[20,64,128]{2,1,0:T(8,128)S(1)}, s32[]{:T(128)}, f32[4,20]{1,0:T(4,128)S(1)}, f32[4,20,64,128]{3,2,1,0:T(8,128)}, /*index=5*/s32[]{:T(128)}, s32[]{:T(128)}, s32[]{:T(128)}, s32[]{:T(128)}) while((s32[]{:T(128)}, f32[20,64,128]{2,1,0:T(8,128)S(1)}, s32[]{:T(128)}, f32[4,20]{1,0:T(4,128)S(1)}, ...), condition=%wide.region_4.5_spmd.clone, body=%wide.region_3.4_spmd.clone.sunk | while | flops 655368 | bytes 1966487 | solution.py:26
  77.8 1.2 fusion.67
  79.0 1.2 fusion.67
  80.3 1.2 fusion.67
  81.6 1.2 fusion.67
  82.9 50.0 %all-gather.6.cloned.1.call-done = f32[80,64,128]{2,1,0:T(8,128)} async-done(((f32[20,64,128]{2,1,0:T(8,128)}), f32[80,64,128]{2,1,0:T(8,128)}) %all-gather.6.cloned.1.call-update) | async-done | bytes 2621456 | tf_op jit(solution)/shard_map/all_gather | solution.py:13
  132.8 5.1 %while.20 = (s32[]{:T(128)}, f32[20,64,128]{2,1,0:T(8,128)S(1)}, s32[]{:T(128)}, f32[4,20]{1,0:T(4,128)S(1)}, f32[4,20,64,128]{3,2,1,0:T(8,128)}, /*index=5*/s32[]{:T(128)}, s32[]{:T(128)}) while((s32[]{:T(128)}, f32[20,64,128]{2,1,0:T(8,128)S(1)}, s32[]{:T(128)}, f32[4,20]{1,0:T(4,128)S(1)}, f32[4,20,64,128]{3,2,1,0:T(8,128)}, ...), condition=%wide.region_2.3_spmd.clone, body=%wide.region_1.2_spmd.clone.sunk | while | flops 655364 | bytes 1966425 | solution.py:26
  132.8 1.2 fusion.66
  134.1 1.2 fusion.66
  135.4 1.2 fusion.66
  136.6 1.2 fusion.66
  139.4 0.7 fusion.23
  140.6 0.7 fusion.18
  141.3 2.1 %fusion.22 = (f32[20,128]{1,0:T(8,128)S(1)}, f32[20,128]{1,0:T(8,128)S(1)}, f32[20,128]{1,0:T(8,128)S(1)}, f32[128,128]{1,0:T(8,128)S(1)}) fusion(f32[20,128]{1,0:T(8,128)S(1)} %copy-done.4, f32[128,128]{1,0:T(8,128)S(1)} %fusion.50, f32[20,128]{1,0:T(8,128)S(1)} %reduce_window_sum.35, pred[128,128]{1,0:T(8,128)(4,1)S(1)} %iota_compare_fusion, ...), kind=kOutput, calls=%fused_computation.29 | convolution fusion | flops 256549376 | bytes 1181696 | tf_op jit(solution)/shard_map/transpose(jvp())/while/body/eval_jaxpr/checkpoint/hts,shp->thp/dot_general | solution.py:41
  143.6 1.2 convolution_bitcast_fusion.1
  144.8 1.2 reduce_window_sum.36
  146.7 1.2 convolution_bitcast_fusion
  149.1 1.6 fusion.15
  150.7 0.9 copy.29
  151.6 20.5 %reduce-scatter.2.cloned.1.call-done = f32[2,32,128]{2,1,0:T(8,128)} async-done(((f32[2,128,128]{2,1,0:T(8,128)}), f32[2,32,128]{2,1,0:T(8,128)}) %reduce-scatter.2.cloned.1.call-update) | async-done | bytes 32784 | tf_op jit(solution)/shard_map/reduce_scatter | solution.py:126
  (60 shorter events, 7.3 us)
Async XLA Ops:
  7.2 70.6 %all-gather.8.cloned.1.call-start = ((), (), s32[]{:S(2)}) async-start(), calls=%async_computation.4 | async-start | bytes 3276800 | tf_op jit(solution)/shard_map/all_gather | solution.py:13
  19.8 13.3 %copy-start.2 = (bf16[2,128,128]{2,1,0:T(8,128)(2,1)}, bf16[2,128,128]{2,1,0:T(8,128)(2,1)S(1)}, u32[]{:S(2)}) copy-start(bf16[2,128,128]{2,1,0:T(8,128)(2,1)S(1)} %all_gather.22) | copy-start | bytes 196612
  21.0 1.4 copy-start.3
  23.2 9.0 %all-to-all-start = ((bf16[4,32,1280]{2,1,0:T(8,128)(2,1)}), bf16[4,32,1280]{2,1,0:T(8,128)(2,1)S(1)}, u32[]{:S(2)}, u32[]{:S(2)}) async-start(bf16[4,32,1280]{2,1,0:T(8,128)(2,1)} %pad_maximum_fusion), calls=%async_computation | async-start | bytes 655360 | tf_op jit(solution)/shard_map/all_to_all | solution.py:85
  26.6 106.2 %all-gather.6.cloned.1.call-start = ((), (), s32[]{:S(2)}) async-start(), calls=%async_computation.3 | async-start | bytes 3276800 | tf_op jit(solution)/shard_map/all_gather | solution.py:13
  32.2 0.9 copy-start
  33.1 2.2 %copy-start.7 = (u32[32]{0:T(128)S(1)}, u32[32]{0:T(128)}, u32[]{:S(2)}) copy-start(u32[32]{0:T(128)} %constant.131) | copy-start | bytes 388
  35.2 137.0 %reduce-scatter.2.cloned.1.call-start = ((), (), s32[]{:S(2)}) async-start(), calls=%async_computation.2 | async-start | bytes 163840 | tf_op jit(solution)/shard_map/reduce_scatter | solution.py:126
  137.9 0.7 copy-start.5
  137.9 0.7 copy-start.4
  137.9 1.1 copy-start.1
  144.8 4.3 %copy-start.6 = (f32[20]{0:T(128)S(1)}, f32[20]{0:T(128)}, u32[]{:S(2)}) copy-start(f32[20]{0:T(128)} %param.14) | copy-start | bytes 244
Sparse Core Ops, SparseCore 0:
  22.5 55.2 all-gather.7
  79.3 53.4 all-gather.5
  149.2 22.8 reduce-scatter.1
